TPU v7x, 32 devices: a whole 2x2x4 slice. The times are simulated.
32 devices in a mesh: cls: 8 (over z, x), dp: 4 (over y, core).
Axes of the slice: x: 2, y: 2, z: 4, core: 2. Of those that a mesh axis runs over, the one named last changes fastest.
Arguments:
- embeddings: bfloat16 [256, 512], P(('dp', 'cls')), parts along dimension 0, may hold values from -4.4194174 to 4.4194174
- labels: int32 [256], P(('dp', 'cls')), parts along dimension 0, may hold values from 0 to 32767
- centers: bfloat16 [131072, 512], P(('dp', 'cls')), parts along dimension 0, may hold values from -3.0935922 to 3.0935922
Outputs:
- losses: float32 [256], P(('dp', 'cls')), parts along dimension 0
- emb_grad: float32 [256, 512], P(('dp', 'cls')), parts along dimension 0
- center_grad: float32 [131072, 512], P(('dp', 'cls')), parts along dimension 0
There are 4 independent parts, one for each index of `dp`. A program takes and returns all parts, laid end to end along the dimension named above; each array names one. Nothing has to cross between parts.
All inputs are finite; a program needn't handle non-finite values.
Results may differ from a plain program's by a relative error of at most 0.0042.
Values may be sent and summed in bfloat16 or wider, within the bound.
A program may use at most 64 MiB of HBM per device.

v0:
```python
import functools
import math

import jax
import jax.numpy as jnp
from jax import lax
from jax.experimental import pallas as pl
from jax.experimental.pallas import tpu as pltpu
from jax.sharding import PartitionSpec as P

logit_scale = 64.0
margin_cosine = math.cos(0.5)
margin_sine = math.sin(0.5)
sine_soften = 0.04
norm_eps = 1e-06
lanes = 128
never = -1e30
log2_e = math.log2(math.e)
MESH = pl.DeviceIdType.MESH
f32 = jnp.float32
bf16 = jnp.bfloat16


def iota(shape, dim):
    return lax.broadcasted_iota(jnp.int32, shape, dim)


def largest_tile(count, limit):
    tile = limit
    while count % tile:
        tile //= 2
    return tile


def gradient_tile(wo_ref, inv_ref, centers_ref, rhs_ref, at):
    repeat = rhs_ref.shape[1] // lanes
    wo = wo_ref[at, :]
    grad = jnp.dot(jnp.concatenate([wo, wo], axis=1), rhs_ref[...], preferred_element_type=f32)
    inverse = inv_ref[at, :]
    centers = centers_ref[at, :].astype(f32)
    along = jnp.sum(centers * grad, axis=1, keepdims=True)
    back = along * (inverse * inverse * inverse)
    return (
        jnp.concatenate([inverse] * repeat, axis=1) * grad
        - jnp.concatenate([back] * repeat, axis=1) * centers
    )


def exchange_kernel(
    n,
    head_tile,
    labels_hbm,
    emb_hbm,
    centers_ref,
    cbuf,
    wo_ref,
    inv_ref,
    rhs_ref,
    fin_ref,
    head_ref,
    hat,
    emb_ref,
    labels_ref,
    xall,
    lall,
    stat,
    stat_in,
    part,
    part_in,
    colst,
    load_sem,
    small_sem,
    x_send,
    x_recv,
    l_send,
    l_recv,
    s_send,
    s_recv,
    p_send,
    p_recv,
):
    me = lax.axis_index("cls")
    own, width = emb_ref.shape
    count = cbuf.shape[0]
    batch = n * own
    wide = 2 * batch
    peers = [lax.rem(me + step, n) for step in range(1, n)]
    sources = [lax.rem(me + n - step, n) for step in range(1, n)]

    barrier = pltpu.get_barrier_semaphore()
    for peer in peers:
        pl.semaphore_signal(barrier, inc=1, device_id={"cls": peer}, device_id_type=MESH)

    small = [
        pltpu.make_async_copy(labels_hbm, labels_ref, small_sem.at[0]),
        pltpu.make_async_copy(emb_hbm, emb_ref, small_sem.at[1]),
    ]
    for copy in small:
        copy.start()
    load = largest_tile(count, 512)
    loads = []
    for k in range(count // load):
        copy = pltpu.make_async_copy(
            centers_ref.at[pl.ds(k * load, load)], cbuf.at[pl.ds(k * load, load)], load_sem.at[k]
        )
        copy.start()
        loads.append(copy)

    for copy in small:
        copy.wait()
    lane = iota((1, wide), 1)
    first = lane - me * own
    label_row = jnp.zeros((1, wide), jnp.int32)
    for i in range(own):
        label_row = jnp.where((first == i) | (first == batch + i), labels_ref[i], label_row)
    lall[me] = label_row
    xall[me] = emb_ref[...]

    def remote(src, dst, send, recv, peer):
        return pltpu.make_async_remote_copy(
            src_ref=src,
            dst_ref=dst,
            send_sem=send,
            recv_sem=recv,
            device_id={"cls": peer},
            device_id_type=MESH,
        )

    pl.semaphore_wait(barrier, n - 1)
    x_copies, l_copies = [], []
    for step, peer in enumerate(peers):
        copy = remote(emb_ref, xall.at[me], x_send.at[step], x_recv.at[step], peer)
        copy.start()
        x_copies.append(copy)
        copy = remote(lall.at[me], lall.at[me], l_send.at[step], l_recv.at[step], peer)
        copy.start()
        l_copies.append(copy)

    sub = largest_tile(load, 64)
    for k in range(count // load):
        loads[k].wait()

        def norm(i, carry):
            at = pl.ds(pl.multiple_of(k * load + i * sub, sub), sub)
            c = cbuf[at, :].astype(f32)
            inverse = lax.rsqrt(jnp.sum(c * c, axis=1, keepdims=True) + norm_eps)
            inv_ref[at, :] = jnp.broadcast_to(inverse, (sub, lanes))
            hat[at, :] = (c * inverse).astype(bf16)
            return carry

        lax.fori_loop(0, load // sub, norm, 0, unroll=2)

    for copy in x_copies + l_copies:
        copy.wait()

    x = jnp.concatenate([xall[j].astype(f32) for j in range(n)], axis=0)
    x_inverse = lax.rsqrt(jnp.sum(x * x, axis=1, keepdims=True) + norm_eps)
    x_hat = (x * x_inverse).astype(bf16)
    x_both = jnp.concatenate([x_hat, x_hat], axis=0)
    label_row = lall[0]
    for j in range(1, n):
        label_row = label_row + lall[j]
    label_row = label_row - me * count
    bias = jnp.where(lane < batch, math.log2(logit_scale) - logit_scale * log2_e, never)
    one_hot_value = jnp.where(lane < batch, 0.0, 1.0)

    tile = largest_tile(count, 512 if wide <= 128 else 128)

    def score(k, carry):
        total, target = carry
        at = pl.ds(pl.multiple_of(k * tile, tile), tile)
        cosine = lax.dot_general(
            hat[at, :], x_both, (((1,), (1,)), ((), ())), preferred_element_type=f32
        )
        mask = iota((tile, wide), 0) == (label_row - k * tile)
        exps = jnp.exp2((logit_scale * log2_e) * cosine + bias)
        values = jnp.where(mask, one_hot_value, exps)
        wo_ref[at, :] = values.astype(bf16)
        picked = jnp.where(mask, cosine, 0.0)
        total = total + jnp.sum(values.reshape(tile // 8, 8, wide), axis=0)
        target = target + jnp.sum(picked.reshape(tile // 8, 8, wide), axis=0)
        return total, target

    zero = jnp.zeros((8, wide), f32)
    total, target = lax.fori_loop(0, count // tile, score, (zero, zero))
    total = jnp.sum(total, axis=0, keepdims=True)
    target = jnp.sum(target, axis=0, keepdims=True)
    stat[...] = jnp.where(lane < batch, total, target)
    s_copies = []
    for step, peer in enumerate(peers):
        copy = remote(stat, stat_in.at[step], s_send.at[step], s_recv.at[step], peer)
        copy.start()
        s_copies.append(copy)

    summed = lax.dot_general(
        wo_ref[...], hat[...], (((0,), (0,)), ((), ())), preferred_element_type=f32
    )
    for j in range(n):
        part[j] = jnp.concatenate(
            [summed[j * own : (j + 1) * own], summed[batch + j * own : batch + (j + 1) * own]],
            axis=0,
        ).astype(bf16)
    p_copies = []
    for step, peer in enumerate(peers):
        copy = remote(part.at[peer], part_in.at[step], p_send.at[step], p_recv.at[step], peer)
        copy.start()
        p_copies.append(copy)

    for copy in s_copies:
        copy.wait()
    sums = stat[...]
    for step in range(n - 1):
        sums = sums + stat_in[step]
    others = sums * (1.0 / logit_scale)
    target_cos = jnp.concatenate([sums[:, batch:], sums[:, :batch]], axis=1)
    target_sine = jnp.sqrt(1.0 + sine_soften - target_cos * target_cos)
    shifted = target_cos * margin_cosine - target_sine * margin_sine
    slope = margin_cosine + margin_sine * target_cos / target_sine
    label_exp = jnp.exp(logit_scale * shifted - logit_scale)
    totals = others + label_exp
    label_weight = (logit_scale * label_exp * slope).astype(bf16).astype(f32)
    losses = jnp.log(totals) + logit_scale - logit_scale * shifted
    stack_row = iota((lanes, wide), 0)
    stack = jnp.where(
        stack_row == 0,
        totals,
        jnp.where(stack_row == 1, slope, jnp.where(stack_row == 2, label_weight, losses)),
    )
    columns = stack.T
    colst[...] = columns[:batch]
    total_col = columns[:batch, 0:1]
    slope_col = columns[:batch, 1:2]
    weight_col = columns[:batch, 2:3]
    x_wide = x_hat.astype(f32)
    scaled = (x_wide / total_col).astype(bf16)
    label_term = weight_col * scaled.astype(f32) - (logit_scale * slope_col) * x_wide
    high = label_term.astype(bf16)
    low = (label_term - high.astype(f32)).astype(bf16)
    rhs_ref[...] = jnp.concatenate([scaled, high, jnp.zeros_like(high), low], axis=0)
    for k in range(head_ref.shape[0] // head_tile):
        at = pl.ds(k * head_tile, head_tile)
        head_ref[at, :] = gradient_tile(wo_ref, inv_ref, cbuf, rhs_ref, at)

    for copy in p_copies:
        copy.wait()
    mine = part[me].astype(f32)
    for step in range(n - 1):
        mine = mine + part_in[step].astype(f32)
    own_col = colst[pl.ds(pl.multiple_of(me * own, own), own), :]
    own_total, own_slope, own_weight = own_col[:, 0:1], own_col[:, 1:2], own_col[:, 2:3]
    picked = mine[own:, :]
    fin_ref[:, :width] = (mine[:own, :] + own_weight * picked) / own_total - (
        logit_scale * own_slope
    ) * picked
    fin_ref[:, width:] = jnp.broadcast_to(own_col[:, 3:4], (own, lanes))


def gradient_kernel(
    tile,
    wo_ref,
    inv_ref,
    centers_ref,
    rhs_ref,
    emb_ref,
    fin_ref,
    head_ref,
    loss_hbm,
    emb_grad_hbm,
    grad_hbm,
    loss_buf,
    emb_grad_buf,
    grad_buf,
    sems,
):
    own, width = emb_ref.shape
    count = wo_ref.shape[0]
    steps = count // tile
    head = head_ref.shape[0] // tile
    stores = []
    for k in range(head):
        at = pl.ds(k * tile, tile)
        copy = pltpu.make_async_copy(head_ref.at[at], grad_hbm.at[at], sems.at[k])
        copy.start()
        stores.append(copy)
    for k in range(head, steps):
        at = pl.ds(k * tile, tile)
        grad_buf[at, :] = gradient_tile(wo_ref, inv_ref, centers_ref, rhs_ref, at)
        copy = pltpu.make_async_copy(grad_buf.at[at], grad_hbm.at[at], sems.at[k])
        copy.start()
        stores.append(copy)
        if k == head:
            x = emb_ref[...].astype(f32)
            inverse = lax.rsqrt(jnp.sum(x * x, axis=1, keepdims=True) + norm_eps)
            units = x * inverse
            grad = fin_ref[:, :width]
            emb_grad_buf[...] = inverse * (
                grad - units * jnp.sum(units * grad, axis=1, keepdims=True)
            )
            loss = fin_ref[:, width:]
            diagonal = iota((own, lanes), 0) == iota((own, lanes), 1)
            loss_row = jnp.sum(jnp.where(diagonal, loss, 0.0), axis=0, keepdims=True)
            loss_buf[...] = loss_row[:, :own]
        if k == min(head + 1, steps - 1):
            for at, (src, dst) in enumerate(((emb_grad_buf, emb_grad_hbm), (loss_buf, loss_hbm))):
                copy = pltpu.make_async_copy(src, dst, sems.at[steps + at])
                copy.start()
                stores.append(copy)
    for copy in stores:
        copy.wait()


def per_device(n, embeddings, labels, centers):
    own, width = embeddings.shape
    count = centers.shape[0]
    batch = n * own
    wide = 2 * batch
    vmem = pl.BlockSpec(memory_space=pltpu.VMEM)
    dma = pltpu.SemaphoreType.DMA
    load = largest_tile(count, 512)
    hbm = pl.BlockSpec(memory_space=pltpu.HBM)
    tile = largest_tile(count, 256)
    head = tile * min(4, count // tile - 1)
    cached, wo, inv, rhs, fin, grad_head = pl.pallas_call(
        functools.partial(exchange_kernel, n, tile),
        out_shape=(
            jax.ShapeDtypeStruct((count, width), bf16),
            jax.ShapeDtypeStruct((count, wide), bf16),
            jax.ShapeDtypeStruct((count, lanes), f32),
            jax.ShapeDtypeStruct((4 * batch, width), bf16),
            jax.ShapeDtypeStruct((own, width + lanes), f32),
            jax.ShapeDtypeStruct((head, width), f32),
        ),
        in_specs=[hbm, hbm, hbm],
        out_specs=(vmem,) * 6,
        scratch_shapes=[
            pltpu.VMEM((count, width), bf16),
            pltpu.VMEM((own, width), bf16),
            pltpu.SMEM((own,), jnp.int32),
            pltpu.VMEM((n, own, width), bf16),
            pltpu.VMEM((n, 1, wide), jnp.int32),
            pltpu.VMEM((1, wide), f32),
            pltpu.VMEM((n - 1, 1, wide), f32),
            pltpu.VMEM((n, 2 * own, width), bf16),
            pltpu.VMEM((n - 1, 2 * own, width), bf16),
            pltpu.VMEM((batch, lanes), f32),
            dma((count // load,)),
            dma((2,)),
        ]
        + [dma((n - 1,))] * 8,
        compiler_params=pltpu.CompilerParams(
            collective_id=0, has_side_effects=True, vmem_limit_bytes=40 * 2**20
        ),
        name="exchange",
    )(*(pltpu.with_memory_space_constraint(v, pltpu.HBM) for v in (labels, embeddings, centers)))

    losses, emb_grad, center_grad = pl.pallas_call(
        functools.partial(gradient_kernel, tile),
        out_shape=(
            jax.ShapeDtypeStruct((1, own), f32),
            jax.ShapeDtypeStruct((own, width), f32),
            jax.ShapeDtypeStruct((count, width), f32),
        ),
        in_specs=[vmem] * 7,
        out_specs=(hbm,) * 3,
        scratch_shapes=[
            pltpu.VMEM((1, own), f32),
            pltpu.VMEM((own, width), f32),
            pltpu.VMEM((count, width), f32),
            dma((count // tile + 2,)),
        ],
        compiler_params=pltpu.CompilerParams(vmem_limit_bytes=32 * 2**20),
        name="gradient",
    )(wo, inv, cached, rhs, embeddings, fin, grad_head)
    return losses.reshape(own), emb_grad, center_grad


def solution(mesh):
    in_specs = (P(("dp", "cls"), None), P(("dp", "cls")), P(("dp", "cls"), None))
    out_specs = (P(("dp", "cls")), P(("dp", "cls"), None), P(("dp", "cls"), None))
    return jax.shard_map(
        functools.partial(per_device, mesh.shape["cls"]),
        mesh=mesh,
        in_specs=in_specs,
        out_specs=out_specs,
        check_vma=False,
    )
```

profile of v0, /device:TPU:0, one launch (start us, length us, event | category | flops | bytes accessed | tf_op | source)
XLA Modules:
  0.0 23.0 jit_solution(7901490651782229052)
XLA Ops:
  0.6 0.0 copy-start
  0.6 18.9 %exchange.1 = (bf16[4096,512]{1,0:T(8,128)(2,1)S(1)}, bf16[4096,128]{1,0:T(8,128)(2,1)S(1)}, f32[4096,128]{1,0:T(8,128)S(1)}, bf16[256,512]{1,0:T(8,128)(2,1)S(1...) custom-call(s32[8]{0:T(128)} %labels_hbm.1, bf16[8,512]{1,0:T(8,128)(2,1)} %emb_ref.1, bf16[4096,512]{1,0:T(8,128)(2,1)} %centers_ref.1), custom_call_target="tpu_custom_call" | custom-call | tf_op jit(solution)/shard_map/exchange/pallas_call | solution.py:323
  19.5 0.0 copy-done
  19.5 3.5 %gradient.1 = (f32[1,8]{1,0:T(1,128)}, f32[8,512]{1,0:T(8,128)}, f32[4096,512]{1,0:T(8,128)}) custom-call(bf16[4096,128]{1,0:T(8,128)(2,1)S(1)} %get-tuple-element.12.wo_ref, f32[4096,128]{1,0:T(8,128)S(1)} %get-tuple-element.13.inv_ref, bf16[4096,512]{1,0:T(8,128)(2,1)S(1)} %get-tuple-element.14.centers_ref, ...), custom_call_target="tpu_custom_call" | custom-call | tf_op jit(solution)/shard_map/gradient/pallas_call | solution.py:356
Async XLA Ops:
  0.6 18.9 %copy-start = (bf16[8,512]{1,0:T(8,128)(2,1)S(1)}, bf16[8,512]{1,0:T(8,128)(2,1)}, u32[]{:S(2)}) copy-start(bf16[8,512]{1,0:T(8,128)(2,1)} %emb_ref.1) | copy-start | bytes 24580
where the time goes:
time: 23.1 us; the launch traced here: 23 us
  Pallas kernels  22.3 us (97%)
  between operations  0.65 us (3%)
    pallas_call x1, Pallas kernels, per_device(): pl.pallas_call(functools.partial(exchange_kernel, n, tile), out_shape=(ja...  18.9 us
    pallas_call x1, Pallas kernels, per_device(): pl.pallas_call(functools.partial(gradient_kernel, tile), out_shape=(jax.S...  3.45 us

commit v1 on v0

--- a/solution.py
+++ b/solution.py
@@ -32,14 +32,31 @@
     return tile
 
 
-def gradient_tile(wo_ref, inv_ref, centers_ref, rhs_ref, at):
-    repeat = rhs_ref.shape[1] // lanes
-    wo = wo_ref[at, :]
-    grad = jnp.dot(jnp.concatenate([wo, wo], axis=1), rhs_ref[...], preferred_element_type=f32)
+def partner(me, n, k):
+    if n & (n - 1):
+        return lax.rem(me + k, n)
+    bit, other = 1, me
+    while bit < n:
+        if k & bit:
+            other = other + bit * (1 - 2 * lax.rem(me // bit, 2))
+        bit *= 2
+    return other
+
+
+def gradient_tile(lhs_ref, inv_ref, centers_ref, rhs_ref, at):
+    width = centers_ref.shape[1]
+    repeat = width // lanes
     inverse = inv_ref[at, :]
     centers = centers_ref[at, :].astype(f32)
-    along = jnp.sum(centers * grad, axis=1, keepdims=True)
-    back = along * (inverse * inverse * inverse)
+    lhs = lhs_ref[at, :]
+    if rhs_ref.shape[1] > width:
+        both = jnp.dot(lhs, rhs_ref[...], preferred_element_type=f32)
+        grad = both[:, :width]
+        back = both[:, width:] * (inverse * inverse)
+    else:
+        grad = jnp.dot(jnp.concatenate([lhs, lhs], axis=1), rhs_ref[...], preferred_element_type=f32)
+        along = jnp.sum(centers * grad, axis=1, keepdims=True)
+        back = along * (inverse * inverse * inverse)
     return (
         jnp.concatenate([inverse] * repeat, axis=1) * grad
         - jnp.concatenate([back] * repeat, axis=1) * centers
@@ -53,10 +70,11 @@
     emb_hbm,
     centers_ref,
     cbuf,
-    wo_ref,
+    lhs_ref,
     inv_ref,
     rhs_ref,
     fin_ref,
+    col_ref,
     head_ref,
     hat,
     emb_ref,
@@ -84,8 +102,8 @@
     count = cbuf.shape[0]
     batch = n * own
     wide = 2 * batch
-    peers = [lax.rem(me + step, n) for step in range(1, n)]
-    sources = [lax.rem(me + n - step, n) for step in range(1, n)]
+    fused = rhs_ref.shape[1] > width
+    peers = [partner(me, n, k) for k in range(n - 1, 0, -1)]
 
     barrier = pltpu.get_barrier_semaphore()
     for peer in peers:
@@ -114,7 +132,8 @@
     for i in range(own):
         label_row = jnp.where((first == i) | (first == batch + i), labels_ref[i], label_row)
     lall[me] = label_row
-    xall[me] = emb_ref[...]
+    x = emb_ref[...].astype(f32)
+    xall[me] = (x * lax.rsqrt(jnp.sum(x * x, axis=1, keepdims=True) + norm_eps)).astype(bf16)
 
     def remote(src, dst, send, recv, peer):
         return pltpu.make_async_remote_copy(
@@ -129,7 +148,7 @@
     pl.semaphore_wait(barrier, n - 1)
     x_copies, l_copies = [], []
     for step, peer in enumerate(peers):
-        copy = remote(emb_ref, xall.at[me], x_send.at[step], x_recv.at[step], peer)
+        copy = remote(xall.at[me], xall.at[me], x_send.at[step], x_recv.at[step], peer)
         copy.start()
         x_copies.append(copy)
         copy = remote(lall.at[me], lall.at[me], l_send.at[step], l_recv.at[step], peer)
@@ -148,14 +167,12 @@
             hat[at, :] = (c * inverse).astype(bf16)
             return carry
 
-        lax.fori_loop(0, load // sub, norm, 0, unroll=2)
+        lax.fori_loop(0, load // sub, norm, 0, unroll=load // sub)
 
     for copy in x_copies + l_copies:
         copy.wait()
 
-    x = jnp.concatenate([xall[j].astype(f32) for j in range(n)], axis=0)
-    x_inverse = lax.rsqrt(jnp.sum(x * x, axis=1, keepdims=True) + norm_eps)
-    x_hat = (x * x_inverse).astype(bf16)
+    x_hat = jnp.concatenate([xall[j] for j in range(n)], axis=0)
     x_both = jnp.concatenate([x_hat, x_hat], axis=0)
     label_row = lall[0]
     for j in range(1, n):
@@ -166,8 +183,7 @@
 
     tile = largest_tile(count, 512 if wide <= 128 else 128)
 
-    def score(k, carry):
-        total, target = carry
+    def score(k, sums):
         at = pl.ds(pl.multiple_of(k * tile, tile), tile)
         cosine = lax.dot_general(
             hat[at, :], x_both, (((1,), (1,)), ((), ())), preferred_element_type=f32
@@ -175,17 +191,18 @@
         mask = iota((tile, wide), 0) == (label_row - k * tile)
         exps = jnp.exp2((logit_scale * log2_e) * cosine + bias)
         values = jnp.where(mask, one_hot_value, exps)
-        wo_ref[at, :] = values.astype(bf16)
-        picked = jnp.where(mask, cosine, 0.0)
-        total = total + jnp.sum(values.reshape(tile // 8, 8, wide), axis=0)
-        target = target + jnp.sum(picked.reshape(tile // 8, 8, wide), axis=0)
-        return total, target
-
-    zero = jnp.zeros((8, wide), f32)
-    total, target = lax.fori_loop(0, count // tile, score, (zero, zero))
-    total = jnp.sum(total, axis=0, keepdims=True)
-    target = jnp.sum(target, axis=0, keepdims=True)
-    stat[...] = jnp.where(lane < batch, total, target)
+        products = values * cosine
+        left = lane < batch
+        lhs_ref[at, :wide] = values.astype(bf16)
+        if fused:
+            lhs_ref[at, wide:] = jnp.where(left, products, values).astype(bf16)
+        counted = jnp.where(left, values, products)
+        return sums + jnp.sum(counted.reshape(tile // 8, 8, wide), axis=0)
+
+    sums = lax.fori_loop(
+        0, count // tile, score, jnp.zeros((8, wide), f32), unroll=count // tile if fused else 1
+    )
+    stat[...] = jnp.sum(sums, axis=0, keepdims=True)
     s_copies = []
     for step, peer in enumerate(peers):
         copy = remote(stat, stat_in.at[step], s_send.at[step], s_recv.at[step], peer)
@@ -193,7 +210,7 @@
         s_copies.append(copy)
 
     summed = lax.dot_general(
-        wo_ref[...], hat[...], (((0,), (0,)), ((), ())), preferred_element_type=f32
+        lhs_ref[:, :wide], hat[...], (((0,), (0,)), ((), ())), preferred_element_type=f32
     )
     for j in range(n):
         part[j] = jnp.concatenate(
@@ -224,7 +241,13 @@
     stack = jnp.where(
         stack_row == 0,
         totals,
-        jnp.where(stack_row == 1, slope, jnp.where(stack_row == 2, label_weight, losses)),
+        jnp.where(
+            stack_row == 1,
+            slope,
+            jnp.where(
+                stack_row == 2, label_weight, jnp.where(stack_row == 3, losses, target_cos)
+            ),
+        ),
     )
     columns = stack.T
     colst[...] = columns[:batch]
@@ -236,33 +259,38 @@
     label_term = weight_col * scaled.astype(f32) - (logit_scale * slope_col) * x_wide
     high = label_term.astype(bf16)
     low = (label_term - high.astype(f32)).astype(bf16)
-    rhs_ref[...] = jnp.concatenate([scaled, high, jnp.zeros_like(high), low], axis=0)
+    rhs_ref[:, :width] = jnp.concatenate([scaled, high, jnp.zeros_like(high), low], axis=0)
+    if fused:
+        inverse = 1.0 / total_col
+        dot = (weight_col * inverse - logit_scale * slope_col) * columns[:batch, 4:5]
+        dot_high = dot.astype(bf16)
+        dot_low = (dot - dot_high.astype(f32)).astype(bf16)
+        rhs_ref[:, width:] = jnp.broadcast_to(
+            jnp.concatenate([jnp.zeros_like(dot_high), dot_high, inverse.astype(bf16), dot_low], axis=0),
+            (4 * batch, lanes),
+        )
+    col_ref[...] = colst[pl.ds(pl.multiple_of(me * own, own), own), :]
     for k in range(head_ref.shape[0] // head_tile):
         at = pl.ds(k * head_tile, head_tile)
-        head_ref[at, :] = gradient_tile(wo_ref, inv_ref, cbuf, rhs_ref, at)
+        head_ref[at, :] = gradient_tile(lhs_ref, inv_ref, cbuf, rhs_ref, at)
 
     for copy in p_copies:
         copy.wait()
     mine = part[me].astype(f32)
     for step in range(n - 1):
         mine = mine + part_in[step].astype(f32)
-    own_col = colst[pl.ds(pl.multiple_of(me * own, own), own), :]
-    own_total, own_slope, own_weight = own_col[:, 0:1], own_col[:, 1:2], own_col[:, 2:3]
-    picked = mine[own:, :]
-    fin_ref[:, :width] = (mine[:own, :] + own_weight * picked) / own_total - (
-        logit_scale * own_slope
-    ) * picked
-    fin_ref[:, width:] = jnp.broadcast_to(own_col[:, 3:4], (own, lanes))
+    fin_ref[...] = mine
 
 
 def gradient_kernel(
     tile,
-    wo_ref,
+    lhs_ref,
     inv_ref,
     centers_ref,
     rhs_ref,
     emb_ref,
     fin_ref,
+    col_ref,
     head_ref,
     loss_hbm,
     emb_grad_hbm,
@@ -273,7 +301,7 @@
     sems,
 ):
     own, width = emb_ref.shape
-    count = wo_ref.shape[0]
+    count = lhs_ref.shape[0]
     steps = count // tile
     head = head_ref.shape[0] // tile
     stores = []
@@ -284,7 +312,7 @@
         stores.append(copy)
     for k in range(head, steps):
         at = pl.ds(k * tile, tile)
-        grad_buf[at, :] = gradient_tile(wo_ref, inv_ref, centers_ref, rhs_ref, at)
+        grad_buf[at, :] = gradient_tile(lhs_ref, inv_ref, centers_ref, rhs_ref, at)
         copy = pltpu.make_async_copy(grad_buf.at[at], grad_hbm.at[at], sems.at[k])
         copy.start()
         stores.append(copy)
@@ -292,11 +320,13 @@
             x = emb_ref[...].astype(f32)
             inverse = lax.rsqrt(jnp.sum(x * x, axis=1, keepdims=True) + norm_eps)
             units = x * inverse
-            grad = fin_ref[:, :width]
+            total, slope, weight = (col_ref[:, at : at + 1] for at in range(3))
+            picked = fin_ref[own:, :]
+            grad = (fin_ref[:own, :] + weight * picked) / total - (logit_scale * slope) * picked
             emb_grad_buf[...] = inverse * (
                 grad - units * jnp.sum(units * grad, axis=1, keepdims=True)
             )
-            loss = fin_ref[:, width:]
+            loss = jnp.broadcast_to(col_ref[:, 3:4], (own, lanes))
             diagonal = iota((own, lanes), 0) == iota((own, lanes), 1)
             loss_row = jnp.sum(jnp.where(diagonal, loss, 0.0), axis=0, keepdims=True)
             loss_buf[...] = loss_row[:, :own]
@@ -319,19 +349,21 @@
     load = largest_tile(count, 512)
     hbm = pl.BlockSpec(memory_space=pltpu.HBM)
     tile = largest_tile(count, 256)
+    fused = wide == lanes
     head = tile * min(4, count // tile - 1)
-    cached, wo, inv, rhs, fin, grad_head = pl.pallas_call(
+    cached, lhs, inv, rhs, fin, col, grad_head = pl.pallas_call(
         functools.partial(exchange_kernel, n, tile),
         out_shape=(
             jax.ShapeDtypeStruct((count, width), bf16),
-            jax.ShapeDtypeStruct((count, wide), bf16),
+            jax.ShapeDtypeStruct((count, 2 * wide if fused else wide), bf16),
             jax.ShapeDtypeStruct((count, lanes), f32),
-            jax.ShapeDtypeStruct((4 * batch, width), bf16),
-            jax.ShapeDtypeStruct((own, width + lanes), f32),
+            jax.ShapeDtypeStruct((4 * batch, width + lanes if fused else width), bf16),
+            jax.ShapeDtypeStruct((2 * own, width), f32),
+            jax.ShapeDtypeStruct((own, lanes), f32),
             jax.ShapeDtypeStruct((head, width), f32),
         ),
         in_specs=[hbm, hbm, hbm],
-        out_specs=(vmem,) * 6,
+        out_specs=(vmem,) * 7,
         scratch_shapes=[
             pltpu.VMEM((count, width), bf16),
             pltpu.VMEM((own, width), bf16),
@@ -360,7 +392,7 @@
             jax.ShapeDtypeStruct((own, width), f32),
             jax.ShapeDtypeStruct((count, width), f32),
         ),
-        in_specs=[vmem] * 7,
+        in_specs=[vmem] * 8,
         out_specs=(hbm,) * 3,
         scratch_shapes=[
             pltpu.VMEM((1, own), f32),
@@ -370,7 +402,7 @@
         ],
         compiler_params=pltpu.CompilerParams(vmem_limit_bytes=32 * 2**20),
         name="gradient",
-    )(wo, inv, cached, rhs, embeddings, fin, grad_head)
+    )(lhs, inv, cached, rhs, embeddings, fin, col, grad_head)
     return losses.reshape(own), emb_grad, center_grad
 
 

time: 23.1 us -> 21.9 us (0.948)
  Pallas kernels: 22.3 us -> 21.1 us
    pallas_call x1, Pallas kernels: 18.9 us -> 17.6 us  [per_device(): pl.pallas_call(functools.partial(exchange_kernel, n, tile), out_shape=(ja...]
where the time goes in v1:
time: 21.9 us; the launch traced here: 21.7 us
  Pallas kernels  21.1 us (96%)
  between operations  0.65 us (3%)
    pallas_call x1, Pallas kernels, per_device(): pl.pallas_call(functools.partial(exchange_kernel, n, tile), out_shape=(ja...  17.6 us
    pallas_call x1, Pallas kernels, per_device(): pl.pallas_call(functools.partial(gradient_kernel, tile), out_shape=(jax.S...  3.46 us

profile of v1, /device:TPU:0, one launch (start us, length us, event | category | flops | bytes accessed | tf_op | source)
XLA Modules:
  0.0 21.7 jit_solution(8909526672849146100)
XLA Ops:
  0.6 0.0 copy-start
  0.6 17.6 %exchange.1 = (bf16[4096,512]{1,0:T(8,128)(2,1)S(1)}, bf16[4096,256]{1,0:T(8,128)(2,1)S(1)}, f32[4096,128]{1,0:T(8,128)S(1)}, bf16[256,640]{1,0:T(8,128)(2,1)S(1...) custom-call(s32[8]{0:T(128)} %labels_hbm.1, bf16[8,512]{1,0:T(8,128)(2,1)} %emb_ref.1, ...), custom_call_target="tpu_custom_call" | custom-call | tf_op jit(solution)/shard_map/exchange/pallas_call | solution.py:354
  18.2 0.0 copy-done
  18.3 3.5 %gradient.1 = (f32[1,8]{1,0:T(1,128)}, f32[8,512]{1,0:T(8,128)}, f32[4096,512]{1,0:T(8,128)}) custom-call(bf16[4096,256]{1,0:T(8,128)(2,1)S(1)} %get-tuple-element.13.lhs_ref, f32[4096,128]{1,0:T(8,128)S(1)} %get-tuple-element.14.inv_ref, bf16[4096,512]{1,0:T(8,128)(2,1)S(1)} %get-tuple-element.15.centers_ref, ...), custom_call_target="tpu_custom_call" | custom-call | tf_op jit(solution)/shard_map/gradient/pallas_call | solution.py:388
Async XLA Ops:
  0.6 17.6 %copy-start = (bf16[8,512]{1,0:T(8,128)(2,1)S(1)}, bf16[8,512]{1,0:T(8,128)(2,1)}, u32[]{:S(2)}) copy-start(bf16[8,512]{1,0:T(8,128)(2,1)} %emb_ref.1) | copy-start | bytes 24580

commit v2 on v1

--- a/solution.py
+++ b/solution.py
@@ -63,7 +63,7 @@
     )
 
 
-def exchange_kernel(
+def exchange_large(
     n,
     head_tile,
     labels_hbm,
@@ -102,7 +102,6 @@
     count = cbuf.shape[0]
     batch = n * own
     wide = 2 * batch
-    fused = rhs_ref.shape[1] > width
     peers = [partner(me, n, k) for k in range(n - 1, 0, -1)]
 
     barrier = pltpu.get_barrier_semaphore()
@@ -192,16 +191,11 @@
         exps = jnp.exp2((logit_scale * log2_e) * cosine + bias)
         values = jnp.where(mask, one_hot_value, exps)
         products = values * cosine
-        left = lane < batch
-        lhs_ref[at, :wide] = values.astype(bf16)
-        if fused:
-            lhs_ref[at, wide:] = jnp.where(left, products, values).astype(bf16)
-        counted = jnp.where(left, values, products)
+        lhs_ref[at, :] = values.astype(bf16)
+        counted = jnp.where(lane < batch, values, products)
         return sums + jnp.sum(counted.reshape(tile // 8, 8, wide), axis=0)
 
-    sums = lax.fori_loop(
-        0, count // tile, score, jnp.zeros((8, wide), f32), unroll=count // tile if fused else 1
-    )
+    sums = lax.fori_loop(0, count // tile, score, jnp.zeros((8, wide), f32))
     stat[...] = jnp.sum(sums, axis=0, keepdims=True)
     s_copies = []
     for step, peer in enumerate(peers):
@@ -210,7 +204,7 @@
         s_copies.append(copy)
 
     summed = lax.dot_general(
-        lhs_ref[:, :wide], hat[...], (((0,), (0,)), ((), ())), preferred_element_type=f32
+        lhs_ref[...], hat[...], (((0,), (0,)), ((), ())), preferred_element_type=f32
     )
     for j in range(n):
         part[j] = jnp.concatenate(
@@ -241,13 +235,7 @@
     stack = jnp.where(
         stack_row == 0,
         totals,
-        jnp.where(
-            stack_row == 1,
-            slope,
-            jnp.where(
-                stack_row == 2, label_weight, jnp.where(stack_row == 3, losses, target_cos)
-            ),
-        ),
+        jnp.where(stack_row == 1, slope, jnp.where(stack_row == 2, label_weight, losses)),
     )
     columns = stack.T
     colst[...] = columns[:batch]
@@ -259,16 +247,7 @@
     label_term = weight_col * scaled.astype(f32) - (logit_scale * slope_col) * x_wide
     high = label_term.astype(bf16)
     low = (label_term - high.astype(f32)).astype(bf16)
-    rhs_ref[:, :width] = jnp.concatenate([scaled, high, jnp.zeros_like(high), low], axis=0)
-    if fused:
-        inverse = 1.0 / total_col
-        dot = (weight_col * inverse - logit_scale * slope_col) * columns[:batch, 4:5]
-        dot_high = dot.astype(bf16)
-        dot_low = (dot - dot_high.astype(f32)).astype(bf16)
-        rhs_ref[:, width:] = jnp.broadcast_to(
-            jnp.concatenate([jnp.zeros_like(dot_high), dot_high, inverse.astype(bf16), dot_low], axis=0),
-            (4 * batch, lanes),
-        )
+    rhs_ref[...] = jnp.concatenate([scaled, high, jnp.zeros_like(high), low], axis=0)
     col_ref[...] = colst[pl.ds(pl.multiple_of(me * own, own), own), :]
     for k in range(head_ref.shape[0] // head_tile):
         at = pl.ds(k * head_tile, head_tile)
@@ -280,6 +259,220 @@
     for step in range(n - 1):
         mine = mine + part_in[step].astype(f32)
     fin_ref[...] = mine
+
+
+def total_wait(ref, sem):
+    pltpu.make_async_copy(ref, ref, sem).wait()
+
+
+def swap_halves(row):
+    half = row.shape[1] // 2
+    return jnp.concatenate([row[:, half:], row[:, :half]], axis=1)
+
+
+def margin_terms(sums):
+    target_cos = swap_halves(sums)
+    target_sine = jnp.sqrt(1.0 + sine_soften - target_cos * target_cos)
+    shifted = target_cos * margin_cosine - target_sine * margin_sine
+    slope = margin_cosine + margin_sine * target_cos / target_sine
+    label_exp = jnp.exp(logit_scale * shifted - logit_scale)
+    total = sums * (1.0 / logit_scale) + label_exp
+    label_weight = (logit_scale * label_exp * slope).astype(bf16).astype(f32)
+    return target_cos, shifted, slope, label_weight, total
+
+
+def exchange_small(
+    n,
+    head_tile,
+    labels_hbm,
+    emb_hbm,
+    centers_ref,
+    cbuf,
+    lhs_ref,
+    inv_ref,
+    rhs_ref,
+    fin_ref,
+    sums_ref,
+    head_ref,
+    hat,
+    hat_t,
+    w_t,
+    emb_ref,
+    labels_ref,
+    xall,
+    lall,
+    stat,
+    stat_in,
+    part,
+    part_in,
+    load_sem,
+    small_sem,
+    send_sem,
+    recv_sem,
+):
+    me = lax.axis_index("cls")
+    own, width = emb_ref.shape
+    count = cbuf.shape[0]
+    batch = n * own
+    half = lanes // 2
+    peers = [partner(me, n, k) for k in range(n - 1, 0, -1)]
+
+    barrier = pltpu.get_barrier_semaphore()
+    for peer in peers:
+        pl.semaphore_signal(barrier, inc=1, device_id={"cls": peer}, device_id_type=MESH)
+
+    small = [
+        pltpu.make_async_copy(labels_hbm, labels_ref, small_sem.at[0]),
+        pltpu.make_async_copy(emb_hbm, emb_ref, small_sem.at[1]),
+    ]
+    for copy in small:
+        copy.start()
+    def send(src, dst, kind, peer):
+        pltpu.make_async_remote_copy(
+            src_ref=src,
+            dst_ref=dst,
+            send_sem=send_sem.at[kind],
+            recv_sem=recv_sem.at[kind],
+            device_id={"cls": peer},
+            device_id_type=MESH,
+        ).start()
+
+    for copy in small:
+        copy.wait()
+    load = count // load_sem.shape[0]
+    loads = []
+    for k in range(count // load):
+        at = pl.ds(k * load, load)
+        copy = pltpu.make_async_copy(centers_ref.at[at], cbuf.at[at], load_sem.at[k])
+        copy.start()
+        loads.append(copy)
+
+    label_rows = jnp.zeros((own, lanes), jnp.int32)
+    for i in range(own):
+        label_rows = jnp.where(iota((own, lanes), 0) == i, labels_ref[i], label_rows)
+    lall[me] = label_rows
+    x = emb_ref[...].astype(f32)
+    xall[me] = (x * lax.rsqrt(jnp.sum(x * x, axis=1, keepdims=True) + norm_eps)).astype(bf16)
+
+    pl.semaphore_wait(barrier, n - 1)
+    for peer in peers:
+        send(xall.at[me], xall.at[me], 0, peer)
+        send(lall.at[me], lall.at[me], 1, peer)
+
+    sub = largest_tile(load, 64)
+    turn = largest_tile(load, 512)
+    for k in range(count // load):
+        loads[k].wait()
+        for i in range(load // sub):
+            at = pl.ds(k * load + i * sub, sub)
+            c = cbuf[at, :].astype(f32)
+            inverse = lax.rsqrt(jnp.sum(c * c, axis=1, keepdims=True) + norm_eps)
+            inv_ref[at, :] = jnp.broadcast_to(inverse, (sub, lanes))
+            hat[at, :] = (c * inverse).astype(bf16)
+        for i in range(load // turn):
+            at = pl.ds(k * load + i * turn, turn)
+            hat_t[:, at] = hat[at, :].T
+
+    total_wait(xall.at[pl.ds(0, n - 1)], recv_sem.at[0])
+    total_wait(lall.at[pl.ds(0, n - 1)], recv_sem.at[1])
+
+    x_hat = jnp.concatenate([xall[j] for j in range(n)], axis=0)
+    label_col = jnp.concatenate([lall[j] for j in range(n)], axis=0) - me * count
+    tile = largest_tile(count, 512)
+    label_wide = jnp.concatenate([label_col] * (tile // lanes), axis=1)
+    place = iota((batch, tile), 1)
+
+    def lane_blocks(value):
+        acc = value[:, :lanes]
+        for i in range(1, value.shape[1] // lanes):
+            acc = acc + value[:, i * lanes : (i + 1) * lanes]
+        return acc
+
+    others = jnp.zeros((batch, lanes), f32)
+    picked = jnp.zeros((batch, lanes), f32)
+    for k in range(count // tile):
+        at = pl.ds(k * tile, tile)
+        cosine = jnp.dot(x_hat, hat_t[:, at], preferred_element_type=f32)
+        mask = place == label_wide - k * tile
+        exps = jnp.exp2((logit_scale * log2_e) * cosine + (math.log2(logit_scale) - logit_scale * log2_e))
+        values = jnp.where(mask, 0.0, exps)
+        w_t[:batch, at] = values.astype(bf16)
+        w_t[2 * batch : 3 * batch, at] = (values * cosine).astype(bf16)
+        others = others + lane_blocks(values)
+        picked = picked + lane_blocks(jnp.where(mask, cosine, 0.0))
+    others = jnp.sum(others, axis=1, keepdims=True)
+    picked = jnp.sum(picked, axis=1, keepdims=True)
+    lane = iota((own, lanes), 1)
+    mine = jnp.zeros((own, lanes), f32)
+    for j in range(n):
+        mine = jnp.where(lane == j, others[j * own : (j + 1) * own], mine)
+        mine = jnp.where(lane == half + j, picked[j * own : (j + 1) * own], mine)
+    stat[...] = mine
+    for k, peer in enumerate(peers):
+        send(stat, stat_in.at[k], 2, peer)
+
+    for k in range(count // tile):
+        at = pl.ds(k * tile, tile)
+        one_hot = jnp.where(place == label_wide - k * tile, 1.0, 0.0).astype(bf16)
+        w_t[batch : 2 * batch, at] = one_hot
+        w_t[3 * batch :, at] = one_hot
+    summed = jnp.dot(w_t[: 2 * batch, :], hat[...], preferred_element_type=f32)
+    for j in range(n):
+        part[j] = jnp.concatenate(
+            [summed[j * own : (j + 1) * own], summed[batch + j * own : batch + (j + 1) * own]],
+            axis=0,
+        ).astype(bf16)
+    for k, peer in enumerate(peers):
+        send(part.at[peer], part_in.at[k], 3, peer)
+
+    for k in range(count // tile):
+        at = pl.ds(k * tile, tile)
+        lhs_ref[at, :] = w_t[:, at].T
+
+    total_wait(stat_in, recv_sem.at[2])
+    sums = stat[...]
+    for k in range(n - 1):
+        sums = sums + stat_in[k]
+    sums_ref[...] = sums
+    target_cos, _, slope, label_weight, total = margin_terms(sums)
+
+    def column(value):
+        return jnp.concatenate([value[:, j : j + 1] for j in range(n)], axis=0)
+
+    inverse = 1.0 / total
+    pull = logit_scale * slope
+    dot = (label_weight * inverse - pull) * target_cos
+    inverse_col, pull_col, weight_col, dot_col = (
+        column(v) for v in (inverse, pull, label_weight, dot)
+    )
+    x_wide = x_hat.astype(f32)
+    scaled = (x_wide * inverse_col).astype(bf16)
+    label_term = weight_col * scaled.astype(f32) - pull_col * x_wide
+    high = label_term.astype(bf16)
+    low = (label_term - high.astype(f32)).astype(bf16)
+    dot_high = dot_col.astype(bf16)
+    dot_low = (dot_col - dot_high.astype(f32)).astype(bf16)
+    rhs_ref[:, :width] = jnp.concatenate([scaled, high, jnp.zeros_like(high), low], axis=0)
+    rhs_ref[:, width:] = jnp.concatenate(
+        [
+            jnp.broadcast_to(v, (batch, lanes))
+            for v in (jnp.zeros_like(dot_high), dot_high, inverse_col.astype(bf16), dot_low)
+        ],
+        axis=0,
+    )
+    for k in range(head_ref.shape[0] // head_tile):
+        at = pl.ds(k * head_tile, head_tile)
+        head_ref[at, :] = gradient_tile(lhs_ref, inv_ref, cbuf, rhs_ref, at)
+
+    total_wait(part_in, recv_sem.at[3])
+    mine = part[me].astype(f32)
+    for k in range(n - 1):
+        mine = mine + part_in[k].astype(f32)
+    fin_ref[...] = mine
+    total_wait(xall.at[pl.ds(0, n - 1)], send_sem.at[0])
+    total_wait(lall.at[pl.ds(0, n - 1)], send_sem.at[1])
+    total_wait(stat_in, send_sem.at[2])
+    total_wait(part_in, send_sem.at[3])
 
 
 def gradient_kernel(
@@ -302,41 +495,43 @@
 ):
     own, width = emb_ref.shape
     count = lhs_ref.shape[0]
+    fused = rhs_ref.shape[1] > width
     steps = count // tile
     head = head_ref.shape[0] // tile
-    stores = []
     for k in range(head):
         at = pl.ds(k * tile, tile)
-        copy = pltpu.make_async_copy(head_ref.at[at], grad_hbm.at[at], sems.at[k])
-        copy.start()
-        stores.append(copy)
+        pltpu.make_async_copy(head_ref.at[at], grad_hbm.at[at], sems.at[0]).start()
     for k in range(head, steps):
         at = pl.ds(k * tile, tile)
         grad_buf[at, :] = gradient_tile(lhs_ref, inv_ref, centers_ref, rhs_ref, at)
-        copy = pltpu.make_async_copy(grad_buf.at[at], grad_hbm.at[at], sems.at[k])
-        copy.start()
-        stores.append(copy)
+        pltpu.make_async_copy(grad_buf.at[at], grad_hbm.at[at], sems.at[0]).start()
         if k == head:
             x = emb_ref[...].astype(f32)
             inverse = lax.rsqrt(jnp.sum(x * x, axis=1, keepdims=True) + norm_eps)
             units = x * inverse
-            total, slope, weight = (col_ref[:, at : at + 1] for at in range(3))
+            if fused:
+                here = iota((own, lanes), 1) == lax.axis_index("cls")
+                _, shifted, slope, weight, total = (
+                    jnp.sum(jnp.where(here, v, 0.0), axis=1, keepdims=True)
+                    for v in margin_terms(col_ref[...])
+                )
+                loss = jnp.log(total) + logit_scale - logit_scale * shifted
+            else:
+                total, slope, weight, loss = (col_ref[:, at : at + 1] for at in range(4))
             picked = fin_ref[own:, :]
             grad = (fin_ref[:own, :] + weight * picked) / total - (logit_scale * slope) * picked
             emb_grad_buf[...] = inverse * (
                 grad - units * jnp.sum(units * grad, axis=1, keepdims=True)
             )
-            loss = jnp.broadcast_to(col_ref[:, 3:4], (own, lanes))
             diagonal = iota((own, lanes), 0) == iota((own, lanes), 1)
-            loss_row = jnp.sum(jnp.where(diagonal, loss, 0.0), axis=0, keepdims=True)
+            loss_row = jnp.sum(jnp.where(diagonal, jnp.broadcast_to(loss, (own, lanes)), 0.0), axis=0, keepdims=True)
             loss_buf[...] = loss_row[:, :own]
         if k == min(head + 1, steps - 1):
-            for at, (src, dst) in enumerate(((emb_grad_buf, emb_grad_hbm), (loss_buf, loss_hbm))):
-                copy = pltpu.make_async_copy(src, dst, sems.at[steps + at])
-                copy.start()
-                stores.append(copy)
-    for copy in stores:
-        copy.wait()
+            pltpu.make_async_copy(emb_grad_buf, emb_grad_hbm, sems.at[1]).start()
+            pltpu.make_async_copy(loss_buf, loss_hbm, sems.at[2]).start()
+    total_wait(grad_hbm, sems.at[0])
+    total_wait(emb_grad_hbm, sems.at[1])
+    total_wait(loss_hbm, sems.at[2])
 
 
 def per_device(n, embeddings, labels, centers):
@@ -350,21 +545,29 @@
     hbm = pl.BlockSpec(memory_space=pltpu.HBM)
     tile = largest_tile(count, 256)
     fused = wide == lanes
-    head = tile * min(4, count // tile - 1)
-    cached, lhs, inv, rhs, fin, col, grad_head = pl.pallas_call(
-        functools.partial(exchange_kernel, n, tile),
-        out_shape=(
-            jax.ShapeDtypeStruct((count, width), bf16),
-            jax.ShapeDtypeStruct((count, 2 * wide if fused else wide), bf16),
-            jax.ShapeDtypeStruct((count, lanes), f32),
-            jax.ShapeDtypeStruct((4 * batch, width + lanes if fused else width), bf16),
-            jax.ShapeDtypeStruct((2 * own, width), f32),
-            jax.ShapeDtypeStruct((own, lanes), f32),
-            jax.ShapeDtypeStruct((head, width), f32),
-        ),
-        in_specs=[hbm, hbm, hbm],
-        out_specs=(vmem,) * 7,
-        scratch_shapes=[
+    head = tile * min(1, count // tile - 1)
+    if fused:
+        kernel = exchange_small
+        scratch = [
+            pltpu.VMEM((count, width), bf16),
+            pltpu.VMEM((width, count), bf16),
+            pltpu.VMEM((4 * batch, count), bf16),
+            pltpu.VMEM((own, width), bf16),
+            pltpu.SMEM((own,), jnp.int32),
+            pltpu.VMEM((n, own, width), bf16),
+            pltpu.VMEM((n, own, lanes), jnp.int32),
+            pltpu.VMEM((own, lanes), f32),
+            pltpu.VMEM((n - 1, own, lanes), f32),
+            pltpu.VMEM((n, 2 * own, width), bf16),
+            pltpu.VMEM((n - 1, 2 * own, width), bf16),
+            dma((count // largest_tile(count, 1024),)),
+            dma((2,)),
+            dma((4,)),
+            dma((4,)),
+        ]
+    else:
+        kernel = exchange_large
+        scratch = [
             pltpu.VMEM((count, width), bf16),
             pltpu.VMEM((own, width), bf16),
             pltpu.SMEM((own,), jnp.int32),
@@ -377,8 +580,21 @@
             pltpu.VMEM((batch, lanes), f32),
             dma((count // load,)),
             dma((2,)),
-        ]
-        + [dma((n - 1,))] * 8,
+        ] + [dma((n - 1,))] * 8
+    cached, lhs, inv, rhs, fin, col, grad_head = pl.pallas_call(
+        functools.partial(kernel, n, tile),
+        out_shape=(
+            jax.ShapeDtypeStruct((count, width), bf16),
+            jax.ShapeDtypeStruct((count, 4 * batch if fused else wide), bf16),
+            jax.ShapeDtypeStruct((count, lanes), f32),
+            jax.ShapeDtypeStruct((4 * batch, width + lanes if fused else width), bf16),
+            jax.ShapeDtypeStruct((2 * own, width), f32),
+            jax.ShapeDtypeStruct((own, lanes), f32),
+            jax.ShapeDtypeStruct((head, width), f32),
+        ),
+        in_specs=[hbm, hbm, hbm],
+        out_specs=(vmem,) * 7,
+        scratch_shapes=scratch,
         compiler_params=pltpu.CompilerParams(
             collective_id=0, has_side_effects=True, vmem_limit_bytes=40 * 2**20
         ),
@@ -398,7 +614,7 @@
             pltpu.VMEM((1, own), f32),
             pltpu.VMEM((own, width), f32),
             pltpu.VMEM((count, width), f32),
-            dma((count // tile + 2,)),
+            dma((3,)),
         ],
         compiler_params=pltpu.CompilerParams(vmem_limit_bytes=32 * 2**20),
         name="gradient",

time: 21.9 us -> 20.7 us (0.945)
  Pallas kernels: 21.1 us -> 19.9 us
    pallas_call x1, Pallas kernels: 17.6 us -> 16.4 us  [per_device(): pl.pallas_call(functools.partial(kernel, n, tile), out_shape=(jax.ShapeDt...]
where the time goes in v2:
time: 20.7 us; the launch traced here: 20.5 us
  Pallas kernels  19.9 us (96%)
  between operations  0.65 us (3%)
    pallas_call x1, Pallas kernels, per_device(): pl.pallas_call(functools.partial(kernel, n, tile), out_shape=(jax.ShapeDt...  16.4 us
    pallas_call x1, Pallas kernels, per_device(): pl.pallas_call(functools.partial(gradient_kernel, tile), out_shape=(jax.S...  3.51 us

profile of v2, /device:TPU:0, one launch (start us, length us, event | category | flops | bytes accessed | tf_op | source)
XLA Modules:
  0.0 20.5 jit_solution(1799614676033832365)
XLA Ops:
  0.6 0.0 copy-start
  0.6 16.4 %exchange.1 = (bf16[4096,512]{1,0:T(8,128)(2,1)S(1)}, bf16[4096,256]{1,0:T(8,128)(2,1)S(1)}, f32[4096,128]{1,0:T(8,128)S(1)}, bf16[256,640]{1,0:T(8,128)(2,1)S(1...) custom-call(s32[8]{0:T(128)} %labels_hbm.1, bf16[8,512]{1,0:T(8,128)(2,1)} %emb_ref.1, ...), custom_call_target="tpu_custom_call" | custom-call | tf_op jit(solution)/shard_map/exchange/pallas_call | solution.py:584
  17.0 0.0 copy-done
  17.0 3.5 %gradient.1 = (f32[1,8]{1,0:T(1,128)}, f32[8,512]{1,0:T(8,128)}, f32[4096,512]{1,0:T(8,128)}) custom-call(bf16[4096,256]{1,0:T(8,128)(2,1)S(1)} %get-tuple-element.13.lhs_ref, f32[4096,128]{1,0:T(8,128)S(1)} %get-tuple-element.14.inv_ref, bf16[4096,512]{1,0:T(8,128)(2,1)S(1)} %get-tuple-element.15.centers_ref, ...), custom_call_target="tpu_custom_call" | custom-call | tf_op jit(solution)/shard_map/gradient/pallas_call | solution.py:604
Async XLA Ops:
  0.6 16.4 %copy-start = (bf16[8,512]{1,0:T(8,128)(2,1)S(1)}, bf16[8,512]{1,0:T(8,128)(2,1)}, u32[]{:S(2)}) copy-start(bf16[8,512]{1,0:T(8,128)(2,1)} %emb_ref.1) | copy-start | bytes 24580

commit v3 on v2

--- a/solution.py
+++ b/solution.py
@@ -265,20 +265,13 @@
     pltpu.make_async_copy(ref, ref, sem).wait()
 
 
-def swap_halves(row):
-    half = row.shape[1] // 2
-    return jnp.concatenate([row[:, half:], row[:, :half]], axis=1)
-
-
-def margin_terms(sums):
-    target_cos = swap_halves(sums)
+def margin_terms(target_cos):
     target_sine = jnp.sqrt(1.0 + sine_soften - target_cos * target_cos)
     shifted = target_cos * margin_cosine - target_sine * margin_sine
     slope = margin_cosine + margin_sine * target_cos / target_sine
-    label_exp = jnp.exp(logit_scale * shifted - logit_scale)
-    total = sums * (1.0 / logit_scale) + label_exp
-    label_weight = (logit_scale * label_exp * slope).astype(bf16).astype(f32)
-    return target_cos, shifted, slope, label_weight, total
+    label_exp = jnp.exp(logit_scale * shifted)
+    label_weight = (label_exp * slope).astype(bf16).astype(f32)
+    return shifted, slope, label_exp, label_weight
 
 
 def exchange_small(
@@ -305,6 +298,7 @@
     stat_in,
     part,
     part_in,
+    early_sums,
     load_sem,
     small_sem,
     send_sem,
@@ -347,17 +341,18 @@
         copy.start()
         loads.append(copy)
 
-    label_rows = jnp.zeros((own, lanes), jnp.int32)
+    lane = iota((own, lanes), 1)
+    label_row = jnp.zeros((1, lanes), jnp.int32)
     for i in range(own):
-        label_rows = jnp.where(iota((own, lanes), 0) == i, labels_ref[i], label_rows)
-    lall[me] = label_rows
+        label_row = jnp.where(lane[:1] == i, labels_ref[i], label_row)
+    lall[me] = label_row.astype(f32)
     x = emb_ref[...].astype(f32)
     xall[me] = (x * lax.rsqrt(jnp.sum(x * x, axis=1, keepdims=True) + norm_eps)).astype(bf16)
 
     pl.semaphore_wait(barrier, n - 1)
     for peer in peers:
+        send(lall.at[me], lall.at[me], 3, peer)
         send(xall.at[me], xall.at[me], 0, peer)
-        send(lall.at[me], lall.at[me], 1, peer)
 
     sub = largest_tile(load, 64)
     turn = largest_tile(load, 512)
@@ -373,78 +368,88 @@
             at = pl.ds(k * load + i * turn, turn)
             hat_t[:, at] = hat[at, :].T
 
+    total_wait(lall.at[pl.ds(0, n - 1)], recv_sem.at[3])
     total_wait(xall.at[pl.ds(0, n - 1)], recv_sem.at[0])
-    total_wait(lall.at[pl.ds(0, n - 1)], recv_sem.at[1])
 
     x_hat = jnp.concatenate([xall[j] for j in range(n)], axis=0)
-    label_col = jnp.concatenate([lall[j] for j in range(n)], axis=0) - me * count
-    tile = largest_tile(count, 512)
-    label_wide = jnp.concatenate([label_col] * (tile // lanes), axis=1)
-    place = iota((batch, tile), 1)
-
-    def lane_blocks(value):
-        acc = value[:, :lanes]
-        for i in range(1, value.shape[1] // lanes):
-            acc = acc + value[:, i * lanes : (i + 1) * lanes]
-        return acc
+    diagonal = lane == iota((own, lanes), 0)
+    labels = [jnp.sum(jnp.where(diagonal, lall[j], 0.0), axis=1, keepdims=True) for j in range(n)]
+    label_col = jnp.concatenate(labels, axis=0).astype(jnp.int32) - me * count
+    lane = iota((batch, lanes), 1)
+    ahead = jnp.broadcast_to(label_col, (batch, lanes)) - lane
+    tile = largest_tile(count, 256)
+    blocks = range(tile // lanes)
+
+    def one_hots(first, last):
+        for k in range(first * tile, last * tile, lanes):
+            at = pl.ds(k, lanes)
+            one_hot = jnp.where(ahead == k, 1.0, 0.0).astype(bf16)
+            w_t[batch : 2 * batch, at] = one_hot
+            w_t[3 * batch :, at] = one_hot
 
     others = jnp.zeros((batch, lanes), f32)
     picked = jnp.zeros((batch, lanes), f32)
     for k in range(count // tile):
-        at = pl.ds(k * tile, tile)
-        cosine = jnp.dot(x_hat, hat_t[:, at], preferred_element_type=f32)
-        mask = place == label_wide - k * tile
-        exps = jnp.exp2((logit_scale * log2_e) * cosine + (math.log2(logit_scale) - logit_scale * log2_e))
-        values = jnp.where(mask, 0.0, exps)
-        w_t[:batch, at] = values.astype(bf16)
-        w_t[2 * batch : 3 * batch, at] = (values * cosine).astype(bf16)
-        others = others + lane_blocks(values)
-        picked = picked + lane_blocks(jnp.where(mask, cosine, 0.0))
+        wide_cosine = jnp.dot(
+            x_hat, hat_t[:, k * tile : (k + 1) * tile], preferred_element_type=f32
+        )
+        for i in blocks:
+            at = pl.ds(k * tile + i * lanes, lanes)
+            cosine = wide_cosine[:, i * lanes : (i + 1) * lanes]
+            mask = ahead == k * tile + i * lanes
+            values = jnp.where(mask, 0.0, jnp.exp2((logit_scale * log2_e) * cosine))
+            w_t[:batch, at] = values.astype(bf16)
+            w_t[2 * batch : 3 * batch, at] = (values * cosine).astype(bf16)
+            others = others + values
+            picked = picked + jnp.where(mask, cosine, 0.0)
+    early = count * 4 // 8
+    one_hots(0, early // tile)
+    early_sums[...] = jnp.dot(w_t[: 2 * batch, :early], hat[:early, :], preferred_element_type=f32)
     others = jnp.sum(others, axis=1, keepdims=True)
     picked = jnp.sum(picked, axis=1, keepdims=True)
-    lane = iota((own, lanes), 1)
+    lane = lane[:own]
     mine = jnp.zeros((own, lanes), f32)
     for j in range(n):
         mine = jnp.where(lane == j, others[j * own : (j + 1) * own], mine)
         mine = jnp.where(lane == half + j, picked[j * own : (j + 1) * own], mine)
     stat[...] = mine
     for k, peer in enumerate(peers):
-        send(stat, stat_in.at[k], 2, peer)
-
-    for k in range(count // tile):
-        at = pl.ds(k * tile, tile)
-        one_hot = jnp.where(place == label_wide - k * tile, 1.0, 0.0).astype(bf16)
-        w_t[batch : 2 * batch, at] = one_hot
-        w_t[3 * batch :, at] = one_hot
-    summed = jnp.dot(w_t[: 2 * batch, :], hat[...], preferred_element_type=f32)
+        send(stat, stat_in.at[k], 1, peer)
+
+    total_wait(xall.at[pl.ds(0, n - 1)], send_sem.at[0])
+    total_wait(lall.at[pl.ds(0, n - 1)], send_sem.at[3])
+    one_hots(early // tile, count // tile)
+    summed = early_sums[...] + jnp.dot(
+        w_t[: 2 * batch, early:], hat[early:, :], preferred_element_type=f32
+    )
     for j in range(n):
         part[j] = jnp.concatenate(
             [summed[j * own : (j + 1) * own], summed[batch + j * own : batch + (j + 1) * own]],
             axis=0,
         ).astype(bf16)
     for k, peer in enumerate(peers):
-        send(part.at[peer], part_in.at[k], 3, peer)
+        send(part.at[peer], part_in.at[k], 2, peer)
 
     for k in range(count // tile):
         at = pl.ds(k * tile, tile)
         lhs_ref[at, :] = w_t[:, at].T
 
-    total_wait(stat_in, recv_sem.at[2])
+    total_wait(stat_in, recv_sem.at[1])
     sums = stat[...]
     for k in range(n - 1):
         sums = sums + stat_in[k]
     sums_ref[...] = sums
-    target_cos, _, slope, label_weight, total = margin_terms(sums)
-
-    def column(value):
-        return jnp.concatenate([value[:, j : j + 1] for j in range(n)], axis=0)
-
-    inverse = 1.0 / total
-    pull = logit_scale * slope
-    dot = (label_weight * inverse - pull) * target_cos
-    inverse_col, pull_col, weight_col, dot_col = (
-        column(v) for v in (inverse, pull, label_weight, dot)
+    _, slope, label_exp, label_weight = margin_terms(sums)
+
+    def column(value, first):
+        return jnp.concatenate([value[:, first + j : first + j + 1] for j in range(n)], axis=0)
+
+    others_col = column(sums, 0)
+    exp_col, pull_col, weight_col, target_col = (
+        column(v, half) for v in (label_exp, logit_scale * slope, label_weight, sums)
     )
+    inverse_col = logit_scale / (others_col + exp_col)
+    dot_col = (weight_col * inverse_col - pull_col) * target_col
     x_wide = x_hat.astype(f32)
     scaled = (x_wide * inverse_col).astype(bf16)
     label_term = weight_col * scaled.astype(f32) - pull_col * x_wide
@@ -464,15 +469,13 @@
         at = pl.ds(k * head_tile, head_tile)
         head_ref[at, :] = gradient_tile(lhs_ref, inv_ref, cbuf, rhs_ref, at)
 
-    total_wait(part_in, recv_sem.at[3])
+    total_wait(part_in, recv_sem.at[2])
     mine = part[me].astype(f32)
     for k in range(n - 1):
         mine = mine + part_in[k].astype(f32)
     fin_ref[...] = mine
-    total_wait(xall.at[pl.ds(0, n - 1)], send_sem.at[0])
-    total_wait(lall.at[pl.ds(0, n - 1)], send_sem.at[1])
-    total_wait(stat_in, send_sem.at[2])
-    total_wait(part_in, send_sem.at[3])
+    total_wait(stat_in, send_sem.at[1])
+    total_wait(part_in, send_sem.at[2])
 
 
 def gradient_kernel(
@@ -510,12 +513,16 @@
             inverse = lax.rsqrt(jnp.sum(x * x, axis=1, keepdims=True) + norm_eps)
             units = x * inverse
             if fused:
-                here = iota((own, lanes), 1) == lax.axis_index("cls")
-                _, shifted, slope, weight, total = (
-                    jnp.sum(jnp.where(here, v, 0.0), axis=1, keepdims=True)
-                    for v in margin_terms(col_ref[...])
+                me = lax.axis_index("cls")
+                lane = iota((own, lanes), 1)
+                others, target_cos = (
+                    jnp.sum(jnp.where(lane == at, col_ref[...], 0.0), axis=1, keepdims=True)
+                    for at in (me, me + lanes // 2)
                 )
-                loss = jnp.log(total) + logit_scale - logit_scale * shifted
+                shifted, slope, label_exp, weight = margin_terms(target_cos)
+                total = others + label_exp
+                loss = jnp.log(total) - logit_scale * shifted
+                total = total * (1.0 / logit_scale)
             else:
                 total, slope, weight, loss = (col_ref[:, at : at + 1] for at in range(4))
             picked = fin_ref[own:, :]
@@ -545,7 +552,7 @@
     hbm = pl.BlockSpec(memory_space=pltpu.HBM)
     tile = largest_tile(count, 256)
     fused = wide == lanes
-    head = tile * min(1, count // tile - 1)
+    head = tile * min(2, count // tile - 1)
     if fused:
         kernel = exchange_small
         scratch = [
@@ -555,12 +562,13 @@
             pltpu.VMEM((own, width), bf16),
             pltpu.SMEM((own,), jnp.int32),
             pltpu.VMEM((n, own, width), bf16),
-            pltpu.VMEM((n, own, lanes), jnp.int32),
+            pltpu.VMEM((n, 1, lanes), f32),
             pltpu.VMEM((own, lanes), f32),
             pltpu.VMEM((n - 1, own, lanes), f32),
             pltpu.VMEM((n, 2 * own, width), bf16),
             pltpu.VMEM((n - 1, 2 * own, width), bf16),
-            dma((count // largest_tile(count, 1024),)),
+            pltpu.VMEM((2 * batch, width), f32),
+            dma((4,)),
             dma((2,)),
             dma((4,)),
             dma((4,)),

time: 20.7 us -> 20.3 us (0.981)
  Pallas kernels: 19.9 us -> 19.4 us
    pallas_call x1, Pallas kernels: 16.4 us -> 16.1 us  [per_device(): pl.pallas_call(functools.partial(kernel, n, tile), out_shape=(jax.ShapeDt...]
where the time goes in v3:
time: 20.3 us; the launch traced here: 20.1 us
  Pallas kernels  19.4 us (96%)
  between operations  0.65 us (3%)
    pallas_call x1, Pallas kernels, per_device(): pl.pallas_call(functools.partial(kernel, n, tile), out_shape=(jax.ShapeDt...  16.1 us
    pallas_call x1, Pallas kernels, per_device(): pl.pallas_call(functools.partial(gradient_kernel, tile), out_shape=(jax.S...  3.36 us

profile of v3, /device:TPU:0, one launch (start us, length us, event | category | flops | bytes accessed | tf_op | source)
XLA Modules:
  0.0 20.1 jit_solution(41696637744027442)
XLA Ops:
  0.6 0.0 copy-start
  0.6 16.1 %exchange.1 = (bf16[4096,512]{1,0:T(8,128)(2,1)S(1)}, bf16[4096,256]{1,0:T(8,128)(2,1)S(1)}, f32[4096,128]{1,0:T(8,128)S(1)}, bf16[256,640]{1,0:T(8,128)(2,1)S(1...) custom-call(s32[8]{0:T(128)} %labels_hbm.1, bf16[8,512]{1,0:T(8,128)(2,1)} %emb_ref.1, ...), custom_call_target="tpu_custom_call" | custom-call | tf_op jit(solution)/shard_map/exchange/pallas_call | solution.py:592
  16.7 0.0 copy-done
  16.7 3.4 %gradient.1 = (f32[1,8]{1,0:T(1,128)}, f32[8,512]{1,0:T(8,128)}, f32[4096,512]{1,0:T(8,128)}) custom-call(bf16[4096,256]{1,0:T(8,128)(2,1)S(1)} %get-tuple-element.13.lhs_ref, f32[4096,128]{1,0:T(8,128)S(1)} %get-tuple-element.14.inv_ref, bf16[4096,512]{1,0:T(8,128)(2,1)S(1)} %get-tuple-element.15.centers_ref, ...), custom_call_target="tpu_custom_call" | custom-call | tf_op jit(solution)/shard_map/gradient/pallas_call | solution.py:612
Async XLA Ops:
  0.6 16.1 %copy-start = (bf16[8,512]{1,0:T(8,128)(2,1)S(1)}, bf16[8,512]{1,0:T(8,128)(2,1)}, u32[]{:S(2)}) copy-start(bf16[8,512]{1,0:T(8,128)(2,1)} %emb_ref.1) | copy-start | bytes 24580

commit v4 on v3

--- a/solution.py
+++ b/solution.py
@@ -299,6 +299,7 @@
     part,
     part_in,
     early_sums,
+    sent,
     load_sem,
     small_sem,
     send_sem,
@@ -325,11 +326,16 @@
         pltpu.make_async_remote_copy(
             src_ref=src,
             dst_ref=dst,
-            send_sem=send_sem.at[kind],
+            send_sem=send_sem.at[min(kind, 1)],
             recv_sem=recv_sem.at[kind],
             device_id={"cls": peer},
             device_id_type=MESH,
         ).start()
+
+    def send_in_order(piece, into, kind):
+        for j in range(n - 1):
+            peer = j + (j >= me).astype(jnp.int32)
+            send(piece(peer), into.at[me - (me > peer).astype(jnp.int32)], kind, peer)
 
     for copy in small:
         copy.wait()
@@ -402,7 +408,7 @@
             w_t[2 * batch : 3 * batch, at] = (values * cosine).astype(bf16)
             others = others + values
             picked = picked + jnp.where(mask, cosine, 0.0)
-    early = count * 4 // 8
+    early = count * 3 // 8
     one_hots(0, early // tile)
     early_sums[...] = jnp.dot(w_t[: 2 * batch, :early], hat[:early, :], preferred_element_type=f32)
     others = jnp.sum(others, axis=1, keepdims=True)
@@ -417,7 +423,6 @@
         send(stat, stat_in.at[k], 1, peer)
 
     total_wait(xall.at[pl.ds(0, n - 1)], send_sem.at[0])
-    total_wait(lall.at[pl.ds(0, n - 1)], send_sem.at[3])
     one_hots(early // tile, count // tile)
     summed = early_sums[...] + jnp.dot(
         w_t[: 2 * batch, early:], hat[early:, :], preferred_element_type=f32
@@ -427,8 +432,7 @@
             [summed[j * own : (j + 1) * own], summed[batch + j * own : batch + (j + 1) * own]],
             axis=0,
         ).astype(bf16)
-    for k, peer in enumerate(peers):
-        send(part.at[peer], part_in.at[k], 2, peer)
+    send_in_order(lambda peer: part.at[peer], part_in, 2)
 
     for k in range(count // tile):
         at = pl.ds(k * tile, tile)
@@ -442,7 +446,13 @@
     _, slope, label_exp, label_weight = margin_terms(sums)
 
     def column(value, first):
-        return jnp.concatenate([value[:, first + j : first + j + 1] for j in range(n)], axis=0)
+        return jnp.concatenate(
+            [
+                jnp.broadcast_to(value[:, first + j : first + j + 1], (own, lanes))
+                for j in range(n)
+            ],
+            axis=0,
+        )
 
     others_col = column(sums, 0)
     exp_col, pull_col, weight_col, target_col = (
@@ -451,19 +461,19 @@
     inverse_col = logit_scale / (others_col + exp_col)
     dot_col = (weight_col * inverse_col - pull_col) * target_col
     x_wide = x_hat.astype(f32)
-    scaled = (x_wide * inverse_col).astype(bf16)
-    label_term = weight_col * scaled.astype(f32) - pull_col * x_wide
+    inverse_wide, pull_wide, weight_wide = (
+        jnp.concatenate([v] * (width // lanes), axis=1)
+        for v in (inverse_col, pull_col, weight_col)
+    )
+    scaled = (x_wide * inverse_wide).astype(bf16)
+    label_term = weight_wide * scaled.astype(f32) - pull_wide * x_wide
     high = label_term.astype(bf16)
     low = (label_term - high.astype(f32)).astype(bf16)
     dot_high = dot_col.astype(bf16)
     dot_low = (dot_col - dot_high.astype(f32)).astype(bf16)
     rhs_ref[:, :width] = jnp.concatenate([scaled, high, jnp.zeros_like(high), low], axis=0)
     rhs_ref[:, width:] = jnp.concatenate(
-        [
-            jnp.broadcast_to(v, (batch, lanes))
-            for v in (jnp.zeros_like(dot_high), dot_high, inverse_col.astype(bf16), dot_low)
-        ],
-        axis=0,
+        [jnp.zeros_like(dot_high), dot_high, inverse_col.astype(bf16), dot_low], axis=0
     )
     for k in range(head_ref.shape[0] // head_tile):
         at = pl.ds(k * head_tile, head_tile)
@@ -474,8 +484,7 @@
     for k in range(n - 1):
         mine = mine + part_in[k].astype(f32)
     fin_ref[...] = mine
-    total_wait(stat_in, send_sem.at[1])
-    total_wait(part_in, send_sem.at[2])
+    total_wait(sent, send_sem.at[1])
 
 
 def gradient_kernel(
@@ -568,9 +577,10 @@
             pltpu.VMEM((n, 2 * own, width), bf16),
             pltpu.VMEM((n - 1, 2 * own, width), bf16),
             pltpu.VMEM((2 * batch, width), f32),
+            pltpu.VMEM(((n - 1) * (1 + own + own * width // lanes), 1, lanes), f32),
             dma((4,)),
             dma((2,)),
-            dma((4,)),
+            dma((2,)),
             dma((4,)),
         ]
     else:

time: 20.3 us -> 20.1 us (level)
  no operation moved by 1% of the time
where the time goes in v4:
time: 20.1 us; the launch traced here: 19.9 us
  Pallas kernels  19.2 us (96%)
  between operations  0.65 us (3%)
    pallas_call x1, Pallas kernels, per_device(): pl.pallas_call(functools.partial(kernel, n, tile), out_shape=(jax.ShapeDt...  15.9 us
    pallas_call x1, Pallas kernels, per_device(): pl.pallas_call(functools.partial(gradient_kernel, tile), out_shape=(jax.S...  3.36 us

profile of v4, /device:TPU:0, one launch (start us, length us, event | category | flops | bytes accessed | tf_op | source)
XLA Modules:
  0.0 19.9 jit_solution(15362675502866344113)
XLA Ops:
  0.6 0.0 copy-start
  0.6 15.9 %exchange.1 = (bf16[4096,512]{1,0:T(8,128)(2,1)S(1)}, bf16[4096,256]{1,0:T(8,128)(2,1)S(1)}, f32[4096,128]{1,0:T(8,128)S(1)}, bf16[256,640]{1,0:T(8,128)(2,1)S(1...) custom-call(s32[8]{0:T(128)} %labels_hbm.1, bf16[8,512]{1,0:T(8,128)(2,1)} %emb_ref.1, ...), custom_call_target="tpu_custom_call" | custom-call | tf_op jit(solution)/shard_map/exchange/pallas_call | solution.py:602
  16.5 0.0 copy-done
  16.5 3.4 %gradient.1 = (f32[1,8]{1,0:T(1,128)}, f32[8,512]{1,0:T(8,128)}, f32[4096,512]{1,0:T(8,128)}) custom-call(bf16[4096,256]{1,0:T(8,128)(2,1)S(1)} %get-tuple-element.13.lhs_ref, f32[4096,128]{1,0:T(8,128)S(1)} %get-tuple-element.14.inv_ref, bf16[4096,512]{1,0:T(8,128)(2,1)S(1)} %get-tuple-element.15.centers_ref, ...), custom_call_target="tpu_custom_call" | custom-call | tf_op jit(solution)/shard_map/gradient/pallas_call | solution.py:622
Async XLA Ops:
  0.6 15.9 %copy-start = (bf16[8,512]{1,0:T(8,128)(2,1)S(1)}, bf16[8,512]{1,0:T(8,128)(2,1)}, u32[]{:S(2)}) copy-start(bf16[8,512]{1,0:T(8,128)(2,1)} %emb_ref.1) | copy-start | bytes 24580

commit v5 on v4

--- a/solution.py
+++ b/solution.py
@@ -266,9 +266,10 @@
 
 
 def margin_terms(target_cos):
-    target_sine = jnp.sqrt(1.0 + sine_soften - target_cos * target_cos)
-    shifted = target_cos * margin_cosine - target_sine * margin_sine
-    slope = margin_cosine + margin_sine * target_cos / target_sine
+    sine_squared = 1.0 + sine_soften - target_cos * target_cos
+    sine_inverse = lax.rsqrt(sine_squared)
+    shifted = target_cos * margin_cosine - sine_squared * sine_inverse * margin_sine
+    slope = margin_cosine + margin_sine * target_cos * sine_inverse
     label_exp = jnp.exp(logit_scale * shifted)
     label_weight = (label_exp * slope).astype(bf16).astype(f32)
     return shifted, slope, label_exp, label_weight
@@ -559,7 +560,7 @@
     dma = pltpu.SemaphoreType.DMA
     load = largest_tile(count, 512)
     hbm = pl.BlockSpec(memory_space=pltpu.HBM)
-    tile = largest_tile(count, 256)
+    tile = largest_tile(count, 128)
     fused = wide == lanes
     head = tile * min(2, count // tile - 1)
     if fused:
@@ -578,7 +579,7 @@
             pltpu.VMEM((n - 1, 2 * own, width), bf16),
             pltpu.VMEM((2 * batch, width), f32),
             pltpu.VMEM(((n - 1) * (1 + own + own * width // lanes), 1, lanes), f32),
-            dma((4,)),
+            dma((2,)),
             dma((2,)),
             dma((2,)),
             dma((4,)),

time: 20.1 us -> 20.1 us (level)
  no operation moved by 1% of the time
where the time goes in v5:
time: 20.1 us; the launch traced here: 19.9 us
  Pallas kernels  19.2 us (96%)
  between operations  0.65 us (3%)
    pallas_call x1, Pallas kernels, per_device(): pl.pallas_call(functools.partial(kernel, n, tile), out_shape=(jax.ShapeDt...  15.8 us
    pallas_call x1, Pallas kernels, per_device(): pl.pallas_call(functools.partial(gradient_kernel, tile), out_shape=(jax.S...  3.4 us

profile of v5, /device:TPU:0, one launch (start us, length us, event | category | flops | bytes accessed | tf_op | source)
XLA Modules:
  0.0 19.9 jit_solution(761470309880620459)
XLA Ops:
  0.6 0.0 copy-start
  0.6 15.8 %exchange.1 = (bf16[4096,512]{1,0:T(8,128)(2,1)S(1)}, bf16[4096,256]{1,0:T(8,128)(2,1)S(1)}, f32[4096,128]{1,0:T(8,128)S(1)}, bf16[256,640]{1,0:T(8,128)(2,1)S(1...) custom-call(s32[8]{0:T(128)} %labels_hbm.1, bf16[8,512]{1,0:T(8,128)(2,1)} %emb_ref.1, ...), custom_call_target="tpu_custom_call" | custom-call | tf_op jit(solution)/shard_map/exchange/pallas_call | solution.py:603
  16.5 0.0 copy-done
  16.5 3.4 %gradient.1 = (f32[1,8]{1,0:T(1,128)}, f32[8,512]{1,0:T(8,128)}, f32[4096,512]{1,0:T(8,128)}) custom-call(bf16[4096,256]{1,0:T(8,128)(2,1)S(1)} %get-tuple-element.13.lhs_ref, f32[4096,128]{1,0:T(8,128)S(1)} %get-tuple-element.14.inv_ref, bf16[4096,512]{1,0:T(8,128)(2,1)S(1)} %get-tuple-element.15.centers_ref, ...), custom_call_target="tpu_custom_call" | custom-call | tf_op jit(solution)/shard_map/gradient/pallas_call | solution.py:623
Async XLA Ops:
  0.6 15.9 %copy-start = (bf16[8,512]{1,0:T(8,128)(2,1)S(1)}, bf16[8,512]{1,0:T(8,128)(2,1)}, u32[]{:S(2)}) copy-start(bf16[8,512]{1,0:T(8,128)(2,1)} %emb_ref.1) | copy-start | bytes 24580
